TPU v7x, 32 devices: a whole 2x2x4 slice. The times are simulated.
32 devices in a mesh: tmpl: 8 (over y, x, core), grid: 4 (over z).
Axes of the slice: x: 2, y: 2, z: 4, core: 2. Of those that a mesh axis runs over, the one named last changes fastest.
Arguments:
- spectrum: float32 [256, 64, 64, 128], P('tmpl', 'grid'), may hold values from -12 to 12
Outputs:
- best_scores: float32 [4, 64, 64, 64], P(None, 'grid', 'tmpl')
- coherence: float32 [64, 64, 64], P('grid', 'tmpl')
All inputs are finite; a program needn't handle non-finite values.
Results may differ from a plain program's by a relative error of at most 0.0001.
Values sent between devices are 32-bit elements; how exact they have to be, the bound alone decides.
A program may use at most 128 MiB of HBM per device.

v0:
```python
import functools
import math

import jax
import jax.numpy as jnp
import numpy as np
from jax import lax
from jax.experimental import pallas as pl
from jax.experimental.pallas import tpu as pltpu
from jax.sharding import PartitionSpec as P

TOP = 4
KEPT = TOP + 1
SPREAD_FLOOR = 0.25
CHUNKS = 4
BATCH = 8
AHEAD = 4
MB = 256
MESH = pl.DeviceIdType.MESH


def phase_tables(points):
    order = np.arange(points)
    angle = (order[:, None] * order[None, :] % points) * (2.0 * math.pi / points)
    table = np.concatenate([np.cos(angle), -np.sin(angle)], axis=0)
    table = np.kron(np.eye(2), table).astype(np.float32)
    lead = table.astype(jnp.bfloat16)
    rest = (table - lead.astype(np.float32)).astype(jnp.bfloat16)
    return np.concatenate([lead, rest], axis=1)


def order_pair(former, latter):
    return jnp.maximum(former, latter), jnp.minimum(former, latter)


def order_four(values):
    a, b = order_pair(values[0], values[1])
    c, d = order_pair(values[2], values[3])
    a, c = order_pair(a, c)
    b, d = order_pair(b, d)
    b, c = order_pair(b, c)
    return [a, b, c, d]


def merge_four(former, latter):
    a, b, c, d = (jnp.maximum(former[i], latter[TOP - 1 - i]) for i in range(TOP))
    a, c = order_pair(a, c)
    b, d = order_pair(b, d)
    a, b = order_pair(a, b)
    c, d = order_pair(c, d)
    return [a, b, c, d]


def merge_groups(former, latter):
    return merge_four(former[:TOP], latter[:TOP]) + [former[TOP] + latter[TOP]]


def kernel(
    groups, slabs, parts,
    spectrum_ref, table_ref, packed_ref,
    held, table, score, stats, gathered, average, scale, leaders, sibling, merged, arrived,
    held_sem, table_sem, stats_send, stats_recv, pair_send, pair_recv, far_send, far_recv,
):
    local_tmpl, slab_rows, beta_rows, doubled = spectrum_ref.shape
    points = doubled // 2
    half = slab_rows // 2
    chips = groups // 2
    piece = beta_rows // groups
    per_chunk = half // CHUNKS
    cell_count = float(points * points * points)

    place = lax.axis_index("tmpl")
    slab = lax.axis_index("grid")
    chip, core = place // 2, place % 2

    def fetch(number):
        return pltpu.make_async_copy(
            spectrum_ref.at[pl.ds(number * BATCH, BATCH)],
            held.at[pl.ds(number * BATCH, BATCH)],
            held_sem.at[number],
        )

    bring_table = pltpu.make_async_copy(table_ref, table, table_sem)
    bring_table.start()
    for number in range(min(AHEAD, local_tmpl // BATCH)):
        fetch(number).start()

    partner = (2 * chip + 1 - core, slab)
    far = [(2 * ((chip + step) % chips) + core, slab) for step in range(1, chips)]
    near = [(place, (slab + step) % slabs) for step in range(1, slabs)]
    barrier = pltpu.get_barrier_semaphore()
    for device in [partner] + far + near:
        pl.semaphore_signal(barrier, inc=1, device_id=device, device_id_type=MESH)

    bring_table.wait()

    def transform(number, carry):
        fetch(number).wait()

        @pl.when(number + AHEAD < local_tmpl // BATCH)
        def _():
            fetch(number + AHEAD).start()

        base = number * BATCH
        lines = MB // beta_rows
        for index in range(BATCH):
            plain = square = None
            for block in range(half // lines):
                leads, rests = [], []
                for side in range(2):
                    coeffs = held[base + index, pl.ds(side * half + block * lines, lines)].reshape(MB, doubled)
                    lead = coeffs.astype(jnp.bfloat16)
                    leads.append(lead)
                    rests.append((coeffs - lead.astype(jnp.float32)).astype(jnp.bfloat16))
                both = jnp.dot(jnp.concatenate(leads, axis=1), table[...], preferred_element_type=jnp.float32)
                value = both[:, :doubled] + both[:, doubled:] + jnp.dot(jnp.concatenate(rests, axis=1), table[:, :doubled], preferred_element_type=jnp.float32)
                score[base + index, pl.ds(block * lines, lines)] = value.reshape(lines, beta_rows, doubled)
                one = value.reshape(MB // 8, 8, doubled)
                p = jnp.sum(one, axis=0)
                q = jnp.sum(one * one, axis=0)
                plain = p if plain is None else plain + p
                square = q if square is None else square + q
            stats[0, pl.ds(base + index, 1)] = jnp.sum(plain, axis=0, keepdims=True)
            stats[1, pl.ds(base + index, 1)] = jnp.sum(square, axis=0, keepdims=True)
        return carry

    def share_stats(part):
        low, high = parts[part], parts[part + 1]
        return [
            pltpu.make_async_remote_copy(
                src_ref=stats.at[:, pl.ds(low, high - low)],
                dst_ref=gathered.at[step, :, pl.ds(low, high - low)],
                send_sem=stats_send.at[part, step],
                recv_sem=stats_recv.at[part, step],
                device_id=near[step],
                device_id_type=MESH,
            )
            for step in range(slabs - 1)
        ]

    def settle(part):
        low, size = parts[part], parts[part + 1] - parts[part]
        total = stats[:, pl.ds(low, size)]
        for step, copy in enumerate(share_stats(part)):
            copy.wait_recv()
            total = total + gathered[step, :, pl.ds(low, size)]
        total = jnp.sum(total, axis=-1, keepdims=True) / cell_count
        mean = total[0]
        spread = total[1] - mean * mean
        factor = 1.0 / jnp.sqrt(spread + SPREAD_FLOOR)
        average[pl.ds(low, size)] = jnp.broadcast_to(mean, (size, doubled))
        scale[pl.ds(low, size)] = jnp.broadcast_to(factor, (size, doubled))

    def leading(part, chunk):
        low, high = parts[part], parts[part + 1]

        def one_row(row, carry):
            line = chunk * per_chunk + row
            for pair in range(chips):
                window = pl.ds(pair * 2 * piece, 2 * piece)
                running = None
                for base in range(low, high, TOP):
                    values = []
                    for tmpl in range(base, base + TOP):
                        centred = score[tmpl, line, window] - average[pl.ds(tmpl, 1)]
                        values.append(centred * scale[pl.ds(tmpl, 1)])
                    summed = (values[0] + values[1]) + (values[2] + values[3])
                    fresh = order_four(values) + [summed]
                    running = fresh if running is None else merge_groups(running, fresh)
                for side in range(2):
                    rows = slice(side * piece, (side + 1) * piece)
                    mine = [value[rows] for value in running]
                    if part > 0:
                        former = [leaders[chunk, side, pair, rank, row] for rank in range(KEPT)]
                        mine = merge_groups(former, mine)
                    for rank in range(KEPT):
                        leaders[chunk, side, pair, rank, row] = mine[rank]
            return carry

        lax.fori_loop(0, per_chunk, one_row, 0)

    def exchange(chunk):
        return pltpu.make_async_remote_copy(
            src_ref=leaders.at[chunk, 1 - core],
            dst_ref=sibling.at[chunk],
            send_sem=pair_send.at[chunk],
            recv_sem=pair_recv.at[chunk],
            device_id=partner,
            device_id_type=MESH,
        )

    def scatter(chunk):
        return [
            pltpu.make_async_remote_copy(
                src_ref=merged.at[chunk, (chip + step) % chips],
                dst_ref=arrived.at[chunk, step - 1],
                send_sem=far_send.at[chunk, step - 1],
                recv_sem=far_recv.at[chunk, step - 1],
                device_id=far[step - 1],
                device_id_type=MESH,
            )
            for step in range(1, chips)
        ]

    def join_pair(chunk):
        exchange(chunk).wait_recv()
        for pair in range(chips):
            former = [leaders[chunk, core, pair, rank] for rank in range(KEPT)]
            latter = [sibling[chunk, pair, rank] for rank in range(KEPT)]
            for rank, value in enumerate(merge_groups(former, latter)):
                merged[chunk, pair, rank] = value
        for copy in scatter(chunk):
            copy.start()

    def finish(chunk):
        running = [merged[chunk, chip, rank] for rank in range(KEPT)]
        for step, copy in enumerate(scatter(chunk)):
            copy.wait_recv()
            running = merge_groups(
                running, [arrived[chunk, step, rank] for rank in range(KEPT)]
            )
        running[TOP] = running[TOP] / math.sqrt(groups * local_tmpl)
        for rank in range(KEPT):
            packed_ref[rank, pl.ds(chunk * per_chunk, per_chunk)] = running[rank]

    count = len(parts) - 1
    for part in range(count):
        lax.fori_loop(parts[part] // BATCH, parts[part + 1] // BATCH, transform, 0)
        if part == 0:
            pl.semaphore_wait(barrier, 1 + len(far) + len(near))
        for copy in share_stats(part):
            copy.start()
    for part in range(count - 1):
        settle(part)
        for chunk in range(CHUNKS):
            leading(part, chunk)
    settle(count - 1)
    for chunk in range(CHUNKS):
        leading(count - 1, chunk)
        exchange(chunk).start()
        if chunk > 0:
            join_pair(chunk - 1)
    join_pair(CHUNKS - 1)
    for chunk in range(CHUNKS):
        finish(chunk)
    for part in range(count):
        for copy in share_stats(part):
            copy.wait_send()
    for chunk in range(CHUNKS):
        exchange(chunk).wait_send()
        for copy in scatter(chunk):
            copy.wait_send()


def unpack(packed_ref, best_ref, coherence_ref):
    half, points = packed_ref.shape[1], best_ref.shape[-1]
    for side in range(2):
        rows = pl.ds(side * half, half)
        lanes = slice(side * points, (side + 1) * points)
        best_ref[:, rows] = packed_ref[:TOP, :, :, lanes]
        coherence_ref[rows] = packed_ref[TOP, :, :, lanes]


def body(groups, slabs, spectrum):
    local_tmpl, slab_rows, beta_rows, doubled = spectrum.shape
    points = doubled // 2
    half = slab_rows // 2
    chips = groups // 2
    piece = beta_rows // groups
    per_chunk = half // CHUNKS
    parts = (0, local_tmpl // 2, local_tmpl)
    count = len(parts) - 1
    block = (chips, KEPT, per_chunk, piece, doubled)
    f32 = jnp.float32
    dma = pltpu.SemaphoreType.DMA
    packed = pl.pallas_call(
        functools.partial(kernel, groups, slabs, parts),
        out_shape=jax.ShapeDtypeStruct((KEPT, half, piece, doubled), f32),
        in_specs=[pl.BlockSpec(memory_space=pltpu.HBM)] * 2,
        out_specs=pl.BlockSpec(memory_space=pltpu.VMEM),
        scratch_shapes=[
            pltpu.VMEM((local_tmpl, slab_rows, beta_rows, doubled), f32),
            pltpu.VMEM((2 * doubled, 2 * doubled), jnp.bfloat16),
            pltpu.VMEM((local_tmpl, half, beta_rows, doubled), f32),
            pltpu.VMEM((2, local_tmpl, doubled), f32),
            pltpu.VMEM((slabs - 1, 2, local_tmpl, doubled), f32),
            pltpu.VMEM((local_tmpl, doubled), f32),
            pltpu.VMEM((local_tmpl, doubled), f32),
            pltpu.VMEM((CHUNKS, 2) + block, f32),
            pltpu.VMEM((CHUNKS,) + block, f32),
            pltpu.VMEM((CHUNKS,) + block, f32),
            pltpu.VMEM((CHUNKS, chips - 1) + block[1:], f32),
            dma((local_tmpl // BATCH,)),
            dma,
            dma((count, slabs - 1)),
            dma((count, slabs - 1)),
            dma((CHUNKS,)),
            dma((CHUNKS,)),
            dma((CHUNKS, chips - 1)),
            dma((CHUNKS, chips - 1)),
        ],
        compiler_params=pltpu.CompilerParams(
            collective_id=0, has_side_effects=True, vmem_limit_bytes=60 * 1024 * 1024
        ),
    )(spectrum, jnp.asarray(phase_tables(points)))
    return pl.pallas_call(
        unpack,
        out_shape=(
            jax.ShapeDtypeStruct((TOP, slab_rows, piece, points), f32),
            jax.ShapeDtypeStruct((slab_rows, piece, points), f32),
        ),
    )(packed)


def solution(mesh):
    return jax.shard_map(
        functools.partial(body, mesh.shape["tmpl"], mesh.shape["grid"]),
        mesh=mesh,
        in_specs=(P("tmpl", "grid", None, None),),
        out_specs=(P(None, "grid", "tmpl", None), P("grid", "tmpl", None)),
        check_vma=False,
    )
```

profile of v0, /device:TPU:0, one launch (start us, length us, event | category | flops | bytes accessed | tf_op | source)
XLA Modules:
  0.0 30.4 jit_solution(6184560523720159159)
XLA Ops:
  0.6 28.0 %shard_map.41.packed_ref = f32[5,8,8,128]{3,2,1,0:T(8,128)} custom-call(f32[32,16,64,128]{3,2,1,0:T(8,128)} %spectrum_ref.1, bf16[256,256]{1,0:T(8,128)(2,1)} %constant.2.clone.table_ref), custom_call_target="tpu_custom_call" | custom-call | tf_op jit(solution)/shard_map/pallas_call | solution.py:276
  28.7 1.7 %shard_map.42 = (f32[4,16,8,64]{3,2,1,0:T(8,128)}, f32[16,8,64]{2,1,0:T(8,128)}) custom-call(f32[5,8,8,128]{3,2,1,0:T(8,128)} %shard_map.41.packed_ref), custom_call_target="tpu_custom_call" | custom-call | tf_op jit(solution)/shard_map/pallas_call | solution.py:306
where the time goes:
time: 30.7 us; the launch traced here: 30.4 us
  Pallas kernels  29.8 us (97%)
  between operations  0.64 us (2%)
    pallas_call x1, Pallas kernels, body(): pl.pallas_call(functools.partial(kernel, groups, slabs, parts), out_shape...  28 us
    pallas_call x1, Pallas kernels, body(): pl.pallas_call(unpack, out_shape=(jax.ShapeDtypeStruct((TOP, slab_rows, p...  1.73 us

commit v1 on v0

v1 whole, which is shorter than its diff:
```python
import functools
import math

import jax
import jax.numpy as jnp
from jax import lax
from jax.experimental import pallas as pl
from jax.experimental.pallas import tpu as pltpu
from jax.sharding import PartitionSpec as P

TOP = 4
KEPT = TOP + 1
SPREAD_FLOOR = 0.25
CHUNKS = 8
LAG = 6
STEP = 4
TILE = 8
MB = 256
MESH = pl.DeviceIdType.MESH


def fill_table(table):
    doubled = table.shape[0] // 2
    points = doubled // 2
    shape = (doubled, doubled)
    row = lax.broadcasted_iota(jnp.int32, shape, 0)
    lane = lax.broadcasted_iota(jnp.int32, shape, 1)
    turns = (row % points) * (lane % points) + (row // points) * (points // 4)
    turns = (turns + points // 2) % points - points // 2
    phase = jnp.cos(turns.astype(jnp.float32) * (2.0 * math.pi / points))
    lead = phase.astype(jnp.bfloat16).astype(jnp.float32)
    for side in range(2):
        inside = (lane // points) == side
        rows = pl.ds(side * doubled, doubled)
        table[rows, :doubled] = jnp.where(inside, lead, 0.0).astype(jnp.bfloat16)
        table[rows, doubled:] = jnp.where(inside, phase - lead, 0.0).astype(jnp.bfloat16)


def order_pair(former, latter):
    return jnp.maximum(former, latter), jnp.minimum(former, latter)


def order_four(values):
    a, b = order_pair(values[0], values[1])
    c, d = order_pair(values[2], values[3])
    a, c = order_pair(a, c)
    b, d = order_pair(b, d)
    b, c = order_pair(b, c)
    return [a, b, c, d]


def merge_four(former, latter):
    a, b, c, d = (jnp.maximum(former[i], latter[TOP - 1 - i]) for i in range(TOP))
    a, c = order_pair(a, c)
    b, d = order_pair(b, d)
    a, b = order_pair(a, b)
    c, d = order_pair(c, d)
    return [a, b, c, d]


def merge_groups(former, latter):
    return merge_four(former[:TOP], latter[:TOP]) + [former[TOP] + latter[TOP]]


def bits_of(chips):
    return chips.bit_length() - 1


def bit_order(chips, chunk):
    bits = bits_of(chips)
    return [(chunk + phase) % bits for phase in range(bits)]


def shuffled(chips, chunk, chip):
    place = 0
    for bit in bit_order(chips, chunk):
        place = place * 2 + (chip >> bit) % 2
    return place


def kernel(groups, slabs, parts, chunks, spectrum_ref, packed_ref, *scratch):
    local_tmpl, slab_rows, beta_rows, doubled = spectrum_ref.shape
    points = doubled // 2
    half = slab_rows // 2
    chips = groups // 2
    bits = bits_of(chips)
    piece = beta_rows // groups
    per_chunk = half // chunks
    cell_count = float(points * points * points)
    scratch = list(scratch)
    take = scratch.pop
    held, table, score, stats, sent, gathered, average, scale, leaders, sibling = (take(0) for _ in range(10))
    work = [take(0) for _ in range(max(bits, 1))]
    arrived = [take(0) for _ in range(bits)]
    held_sem, stats_send, stats_recv, pair_send, pair_recv, far_send, far_recv = scratch

    place = lax.axis_index("tmpl")
    slab = lax.axis_index("grid")
    chip, core = place // 2, place % 2

    def fetch(number):
        return pltpu.make_async_copy(
            spectrum_ref.at[pl.ds(number * STEP, STEP)],
            held.at[pl.ds(number * STEP, STEP)],
            held_sem.at[number],
        )

    for number in range(local_tmpl // STEP):
        fetch(number).start(priority=1)

    def own_bit(bit):
        return (chip // 2**bit) % 2

    partner = (2 * chip + 1 - core, slab)
    across = [(2 * (chip + 2**bit * (1 - 2 * own_bit(bit))) + core, slab) for bit in range(bits)]
    near = [(place, (slab + step) % slabs) for step in range(1, slabs)]
    barrier = pltpu.get_barrier_semaphore()
    for device in [partner] + across + near:
        pl.semaphore_signal(barrier, inc=1, device_id=device, device_id_type=MESH)

    fill_table(table)

    def transform(number, carry):
        fetch(number).wait()
        base = number * STEP
        lines = MB // beta_rows
        for index in range(STEP):
            plain = square = None
            for block in range(half // lines):
                leads, rests = [], []
                for side in range(2):
                    coeffs = held[base + index, pl.ds(side * half + block * lines, lines)].reshape(MB, doubled)
                    lead = coeffs.astype(jnp.bfloat16)
                    leads.append(lead)
                    rests.append((coeffs - lead.astype(jnp.float32)).astype(jnp.bfloat16))
                both = jnp.dot(jnp.concatenate(leads, axis=1), table[...], preferred_element_type=jnp.float32)
                value = both[:, :doubled] + both[:, doubled:] + jnp.dot(jnp.concatenate(rests, axis=1), table[:, :doubled], preferred_element_type=jnp.float32)
                score[base + index, pl.ds(block * lines, lines)] = value.reshape(lines, beta_rows, doubled)
                one = value.reshape(MB // 8, 8, doubled)
                p = jnp.sum(one, axis=0)
                q = jnp.sum(one * one, axis=0)
                plain = p if plain is None else plain + p
                square = q if square is None else square + q
            stats[0, pl.ds(base + index, 1)] = jnp.sum(plain, axis=0, keepdims=True)
            stats[1, pl.ds(base + index, 1)] = jnp.sum(square, axis=0, keepdims=True)
        return carry

    def slots(part):
        tiles = (parts[part + 1] - parts[part]) // TILE
        width = doubled // (2 * tiles)
        lane = lax.broadcasted_iota(jnp.int32, (TILE, doubled), 1)
        places = [(kind, tile) for tile in range(tiles) for kind in range(2)]
        return [
            (kind, parts[part] + tile * TILE, (lane >= index * width) & (lane < (index + 1) * width), width)
            for index, (kind, tile) in enumerate(places)
        ]

    def share_stats(part):
        return [
            pltpu.make_async_remote_copy(
                src_ref=sent.at[part],
                dst_ref=gathered.at[part, step],
                send_sem=stats_send.at[part, step],
                recv_sem=stats_recv.at[part, step],
                device_id=near[step],
                device_id_type=MESH,
            )
            for step in range(slabs - 1)
        ]

    def publish(part):
        message = jnp.zeros((TILE, doubled), jnp.float32)
        for kind, row, mask, _ in slots(part):
            total = jnp.sum(stats[kind, pl.ds(row, TILE)], axis=-1, keepdims=True)
            message = jnp.where(mask, total, message)
        sent[part] = message
        for copy in share_stats(part):
            copy.start()

    def settle(part):
        total = sent[part]
        for step, copy in enumerate(share_stats(part)):
            copy.wait_recv()
            total = total + gathered[part, step]
        mean = None
        for kind, row, mask, width in slots(part):
            value = jnp.sum(jnp.where(mask, total, 0.0), axis=-1, keepdims=True) * (1.0 / (width * cell_count))
            if kind == 0:
                mean = value
                continue
            factor = 1.0 / jnp.sqrt(value - mean * mean + SPREAD_FLOOR)
            average[pl.ds(row, TILE)] = jnp.broadcast_to(mean, (TILE, doubled))
            scale[pl.ds(row, TILE)] = jnp.broadcast_to(factor, (TILE, doubled))

    def leading(part, chunk):
        low, high = parts[part], parts[part + 1]

        def one_row(row, carry):
            line = chunk * per_chunk + row
            for pair in range(chips):
                window = pl.ds(pair * 2 * piece, 2 * piece)
                running = None
                for base in range(low, high, TOP):
                    values = []
                    for tmpl in range(base, base + TOP):
                        centred = score[tmpl, line, window] - average[pl.ds(tmpl, 1)]
                        values.append(centred * scale[pl.ds(tmpl, 1)])
                    summed = (values[0] + values[1]) + (values[2] + values[3])
                    fresh = order_four(values) + [summed]
                    running = fresh if running is None else merge_groups(running, fresh)
                for side in range(2):
                    rows = slice(side * piece, (side + 1) * piece)
                    mine = [value[rows] for value in running]
                    if part > 0:
                        former = [leaders[chunk, side, pair, rank, row] for rank in range(KEPT)]
                        mine = merge_groups(former, mine)
                    for rank in range(KEPT):
                        leaders[chunk, side, pair, rank, row] = mine[rank]
            return carry

        lax.fori_loop(0, per_chunk, one_row, 0)

    def exchange(chunk):
        return pltpu.make_async_remote_copy(
            src_ref=leaders.at[chunk, 1 - core],
            dst_ref=sibling.at[chunk],
            send_sem=pair_send.at[chunk],
            recv_sem=pair_recv.at[chunk],
            device_id=partner,
            device_id_type=MESH,
        )

    def halving(phase, chunk):
        bit = bit_order(chips, chunk)[phase]
        kept = chips >> (phase + 1)
        return pltpu.make_async_remote_copy(
            src_ref=work[phase].at[chunk, pl.ds((1 - own_bit(bit)) * kept, kept)],
            dst_ref=arrived[phase].at[chunk],
            send_sem=far_send.at[phase, chunk],
            recv_sem=far_recv.at[phase, chunk],
            device_id=across[bit],
            device_id_type=MESH,
        )

    def hand_on(phase, chunk, slot, values):
        if phase < bits:
            for rank in range(KEPT):
                work[phase][chunk, slot, rank] = values[rank]
            return
        values[TOP] = values[TOP] / math.sqrt(groups * local_tmpl)
        for rank in range(KEPT):
            packed_ref[rank, pl.ds(chunk * per_chunk, per_chunk)] = values[rank]

    def join_pair(chunk):
        exchange(chunk).wait_recv()
        for pair in range(chips):
            former = [leaders[chunk, core, pair, rank] for rank in range(KEPT)]
            latter = [sibling[chunk, pair, rank] for rank in range(KEPT)]
            hand_on(0, chunk, shuffled(chips, chunk, pair), merge_groups(former, latter))
        if bits:
            halving(0, chunk).start()

    def join_far(phase, chunk):
        halving(phase, chunk).wait_recv()
        kept = chips >> (phase + 1)
        mine = own_bit(bit_order(chips, chunk)[phase]) * kept
        for slot in range(kept):
            former = [work[phase][chunk, mine + slot, rank] for rank in range(KEPT)]
            latter = [arrived[phase][chunk, slot, rank] for rank in range(KEPT)]
            hand_on(phase + 1, chunk, slot, merge_groups(former, latter))
        if phase + 1 < bits:
            halving(phase + 1, chunk).start()

    count = len(parts) - 1
    for part in range(count):
        lax.fori_loop(parts[part] // STEP, parts[part + 1] // STEP, transform, 0)
        if part == 0:
            pl.semaphore_wait(barrier, 1 + len(across) + len(near))
        publish(part)
    for part in range(count - 1):
        settle(part)
        for chunk in range(chunks):
            leading(part, chunk)
    settle(count - 1)
    for chunk in range(chunks):
        leading(count - 1, chunk)
        exchange(chunk).start()
        if chunk >= LAG:
            join_pair(chunk - LAG)
    for chunk in range(max(chunks - LAG, 0), chunks):
        join_pair(chunk)
    for phase in range(bits):
        for chunk in range(chunks):
            join_far(phase, chunk)
    for part in range(count):
        for copy in share_stats(part):
            copy.wait_send()
    for chunk in range(chunks):
        exchange(chunk).wait_send()
        for phase in range(bits):
            halving(phase, chunk).wait_send()


def unpack(packed_ref, best_ref, coherence_ref):
    half, points = packed_ref.shape[1], best_ref.shape[-1]
    for side in range(2):
        rows = pl.ds(side * half, half)
        lanes = slice(side * points, (side + 1) * points)
        best_ref[:, rows] = packed_ref[:TOP, :, :, lanes]
        coherence_ref[rows] = packed_ref[TOP, :, :, lanes]


def body(groups, slabs, spectrum):
    local_tmpl, slab_rows, beta_rows, doubled = spectrum.shape
    points = doubled // 2
    half = slab_rows // 2
    chips = groups // 2
    bits = bits_of(chips)
    piece = beta_rows // groups
    chunks = min(CHUNKS, half)
    per_chunk = half // chunks
    parts = (0, local_tmpl // 4 * 3, local_tmpl)
    count = len(parts) - 1
    block = (KEPT, per_chunk, piece, doubled)
    f32 = jnp.float32
    dma = pltpu.SemaphoreType.DMA
    packed = pl.pallas_call(
        functools.partial(kernel, groups, slabs, parts, chunks),
        out_shape=jax.ShapeDtypeStruct((KEPT, half, piece, doubled), f32),
        in_specs=[pl.BlockSpec(memory_space=pltpu.HBM)],
        out_specs=pl.BlockSpec(memory_space=pltpu.VMEM),
        scratch_shapes=[
            pltpu.VMEM((local_tmpl, slab_rows, beta_rows, doubled), f32),
            pltpu.VMEM((2 * doubled, 2 * doubled), jnp.bfloat16),
            pltpu.VMEM((local_tmpl, half, beta_rows, doubled), f32),
            pltpu.VMEM((2, local_tmpl, doubled), f32),
            pltpu.VMEM((count, TILE, doubled), f32),
            pltpu.VMEM((count, slabs - 1, TILE, doubled), f32),
            pltpu.VMEM((local_tmpl, doubled), f32),
            pltpu.VMEM((local_tmpl, doubled), f32),
            pltpu.VMEM((chunks, 2, chips) + block, f32),
            pltpu.VMEM((chunks, chips) + block, f32),
        ]
        + [pltpu.VMEM((chunks, chips >> phase) + block, f32) for phase in range(max(bits, 1))]
        + [pltpu.VMEM((chunks, chips >> (phase + 1)) + block, f32) for phase in range(bits)]
        + [
            dma((local_tmpl // STEP,)),
            dma((count, slabs - 1)),
            dma((count, slabs - 1)),
            dma((chunks,)),
            dma((chunks,)),
            dma((max(bits, 1), chunks)),
            dma((max(bits, 1), chunks)),
        ],
        compiler_params=pltpu.CompilerParams(
            collective_id=0, has_side_effects=True, vmem_limit_bytes=48 * 1024 * 1024
        ),
    )(spectrum)
    return pl.pallas_call(
        unpack,
        out_shape=(
            jax.ShapeDtypeStruct((TOP, slab_rows, piece, points), f32),
            jax.ShapeDtypeStruct((slab_rows, piece, points), f32),
        ),
        compiler_params=pltpu.CompilerParams(vmem_limit_bytes=8 * 1024 * 1024),
    )(packed)


def solution(mesh):
    return jax.shard_map(
        functools.partial(body, mesh.shape["tmpl"], mesh.shape["grid"]),
        mesh=mesh,
        in_specs=(P("tmpl", "grid", None, None),),
        out_specs=(P(None, "grid", "tmpl", None), P("grid", "tmpl", None)),
        check_vma=False,
    )
```

time: 30.7 us -> 27.1 us (0.88)
  Pallas kernels: 29.8 us -> 26.3 us
    pallas_call x1, Pallas kernels: 28 us -> 25.5 us  [body(): pl.pallas_call(functools.partial(kernel, groups, slabs, parts, chunks), o...]
    pallas_call x1, Pallas kernels: 1.73 us -> 0.82 us  [body(): pl.pallas_call(unpack, out_shape=(jax.ShapeDtypeStruct((TOP, slab_rows, p...]
where the time goes in v1:
time: 27.1 us; the launch traced here: 26.9 us
  Pallas kernels  26.3 us (97%)
  between operations  0.64 us (2%)
    pallas_call x1, Pallas kernels, body(): pl.pallas_call(functools.partial(kernel, groups, slabs, parts, chunks), o...  25.5 us
    pallas_call x1, Pallas kernels, body(): pl.pallas_call(unpack, out_shape=(jax.ShapeDtypeStruct((TOP, slab_rows, p...  0.82 us

profile of v1, /device:TPU:0, one launch (start us, length us, event | category | flops | bytes accessed | tf_op | source)
XLA Modules:
  0.0 26.9 jit_solution(7571484095065211483)
XLA Ops:
  0.6 25.5 %shard_map.30.packed_ref = f32[5,8,8,128]{3,2,1,0:T(8,128)S(1)} custom-call(f32[32,16,64,128]{3,2,1,0:T(8,128)} %spectrum_ref.1), custom_call_target="tpu_custom_call" | custom-call | tf_op jit(solution)/shard_map/pallas_call | solution.py:327
  26.1 0.8 %shard_map.31 = (f32[4,16,8,64]{3,2,1,0:T(8,128)}, f32[16,8,64]{2,1,0:T(8,128)}) custom-call(f32[5,8,8,128]{3,2,1,0:T(8,128)S(1)} %shard_map.30.packed_ref), custom_call_target="tpu_custom_call" | custom-call | tf_op jit(solution)/shard_map/pallas_call | solution.py:359

commit v2 on v1

--- a/solution.py
+++ b/solution.py
@@ -12,7 +12,7 @@
 KEPT = TOP + 1
 SPREAD_FLOOR = 0.25
 CHUNKS = 8
-LAG = 6
+HALVED = 4
 STEP = 4
 TILE = 8
 MB = 256
@@ -89,10 +89,19 @@
     cell_count = float(points * points * points)
     scratch = list(scratch)
     take = scratch.pop
-    held, table, score, stats, sent, gathered, average, scale, leaders, sibling = (take(0) for _ in range(10))
+    held, table, score, stats, sent, gathered, average, scale, leaders, sibling, extra, told = (take(0) for _ in range(12))
     work = [take(0) for _ in range(max(bits, 1))]
     arrived = [take(0) for _ in range(bits)]
-    held_sem, stats_send, stats_recv, pair_send, pair_recv, far_send, far_recv = scratch
+    landed = take(0)
+    halved = min(HALVED, chunks // 2)
+    (
+        held_sem, stats_send, stats_recv, told_send, told_recv, raw_send, raw_recv,
+        pair_send, pair_recv, half_send, half_recv, far_send, far_recv,
+    ) = scratch
+    count = len(parts) - 1
+    late = parts[count - 1]
+    late_size = local_tmpl - late
+    aligned = piece % TILE == 0
 
     place = lax.axis_index("tmpl")
     slab = lax.axis_index("grid")
@@ -113,9 +122,11 @@
 
     partner = (2 * chip + 1 - core, slab)
     across = [(2 * (chip + 2**bit * (1 - 2 * own_bit(bit))) + core, slab) for bit in range(bits)]
+    far = [(2 * ((chip + step) % chips) + core, slab) for step in range(1, chips)]
     near = [(place, (slab + step) % slabs) for step in range(1, slabs)]
+    beside = [(2 * chip + 1 - core, (slab + step) % slabs) for step in range(slabs)]
     barrier = pltpu.get_barrier_semaphore()
-    for device in [partner] + across + near:
+    for device in far + near + beside:
         pl.semaphore_signal(barrier, inc=1, device_id=device, device_id_type=MESH)
 
     fill_table(table)
@@ -177,11 +188,35 @@
         for copy in share_stats(part):
             copy.start()
 
-    def settle(part):
-        total = sent[part]
-        for step, copy in enumerate(share_stats(part)):
-            copy.wait_recv()
-            total = total + gathered[part, step]
+    def tell_late():
+        return [
+            pltpu.make_async_remote_copy(
+                src_ref=sent.at[count - 1],
+                dst_ref=told.at[step],
+                send_sem=told_send.at[step],
+                recv_sem=told_recv.at[step],
+                device_id=beside[step],
+                device_id_type=MESH,
+            )
+            for step in range(slabs)
+        ]
+
+    def raw(number, owner):
+        base = number * STEP
+        spans = [(pair * 2 * piece + owner * piece, piece) for pair in range(chips)] if aligned else [(0, beta_rows)]
+        return [
+            pltpu.make_async_remote_copy(
+                src_ref=score.at[pl.ds(base, STEP), :, pl.ds(pl.multiple_of(start, TILE), size)],
+                dst_ref=extra.at[pl.ds(base - late, STEP), :, pl.ds(pl.multiple_of(start, TILE), size)],
+                send_sem=raw_send.at[number - late // STEP, index],
+                recv_sem=raw_recv.at[number - late // STEP, index],
+                device_id=partner,
+                device_id_type=MESH,
+            )
+            for index, (start, size) in enumerate(spans)
+        ]
+
+    def spread_out(part, total, shift):
         mean = None
         for kind, row, mask, width in slots(part):
             value = jnp.sum(jnp.where(mask, total, 0.0), axis=-1, keepdims=True) * (1.0 / (width * cell_count))
@@ -189,8 +224,52 @@
                 mean = value
                 continue
             factor = 1.0 / jnp.sqrt(value - mean * mean + SPREAD_FLOOR)
-            average[pl.ds(row, TILE)] = jnp.broadcast_to(mean, (TILE, doubled))
-            scale[pl.ds(row, TILE)] = jnp.broadcast_to(factor, (TILE, doubled))
+            average[pl.ds(row + shift, TILE)] = jnp.broadcast_to(mean, (TILE, doubled))
+            scale[pl.ds(row + shift, TILE)] = jnp.broadcast_to(factor, (TILE, doubled))
+
+    def settle(part):
+        for copy in share_stats(part):
+            copy.wait_recv()
+        if part == count - 1:
+            for copy in tell_late():
+                copy.wait_recv()
+        total = sent[part]
+        for step in range(slabs - 1):
+            total = total + gathered[part, step]
+        if part == count - 1:
+            spread_out(part, sum((told[step] for step in range(1, slabs)), told[0]), late_size)
+        spread_out(part, total, 0)
+
+    def gather_up(running, values):
+        summed = (values[0] + values[1]) + (values[2] + values[3])
+        fresh = order_four(values) + [summed]
+        return fresh if running is None else merge_groups(running, fresh)
+
+    def last_leading(chunk):
+        for row in range(per_chunk):
+            line = chunk * per_chunk + row
+            for pair in range(chips):
+                start = pl.multiple_of(pair * 2 * piece + core * piece, piece)
+                window = pl.ds(start, piece)
+                running = None
+                for base in range(late, local_tmpl, TOP):
+                    running = gather_up(running, [
+                        (score[tmpl, line, window] - average[pl.ds(tmpl, 1)]) * scale[pl.ds(tmpl, 1)]
+                        for tmpl in range(base, base + TOP)
+                    ])
+                for base in range(0, late_size, TOP):
+                    running = gather_up(running, [
+                        (extra[tmpl, line, window] - average[pl.ds(local_tmpl + tmpl, 1)]) * scale[pl.ds(local_tmpl + tmpl, 1)]
+                        for tmpl in range(base, base + TOP)
+                    ])
+                former = [leaders[chunk, core, pair, rank, row] for rank in range(KEPT)]
+                latter = [sibling[chunk, pair, rank, row] for rank in range(KEPT)]
+                running = merge_groups(running, merge_groups(former, latter))
+                slot = shuffled(chips, chunk, pair) if chunk < halved else pair
+                for rank in range(KEPT):
+                    work[0][chunk, slot, rank, row] = running[rank]
+        for copy in [halving(0, chunk)] if chunk < halved else scatter(chunk):
+            copy.start()
 
     def leading(part, chunk):
         low, high = parts[part], parts[part + 1]
@@ -201,13 +280,10 @@
                 window = pl.ds(pair * 2 * piece, 2 * piece)
                 running = None
                 for base in range(low, high, TOP):
-                    values = []
-                    for tmpl in range(base, base + TOP):
-                        centred = score[tmpl, line, window] - average[pl.ds(tmpl, 1)]
-                        values.append(centred * scale[pl.ds(tmpl, 1)])
-                    summed = (values[0] + values[1]) + (values[2] + values[3])
-                    fresh = order_four(values) + [summed]
-                    running = fresh if running is None else merge_groups(running, fresh)
+                    running = gather_up(running, [
+                        (score[tmpl, line, window] - average[pl.ds(tmpl, 1)]) * scale[pl.ds(tmpl, 1)]
+                        for tmpl in range(base, base + TOP)
+                    ])
                 for side in range(2):
                     rows = slice(side * piece, (side + 1) * piece)
                     mine = [value[rows] for value in running]
@@ -236,68 +312,107 @@
         return pltpu.make_async_remote_copy(
             src_ref=work[phase].at[chunk, pl.ds((1 - own_bit(bit)) * kept, kept)],
             dst_ref=arrived[phase].at[chunk],
-            send_sem=far_send.at[phase, chunk],
-            recv_sem=far_recv.at[phase, chunk],
+            send_sem=half_send.at[phase, chunk],
+            recv_sem=half_recv.at[phase, chunk],
             device_id=across[bit],
             device_id_type=MESH,
         )
 
-    def hand_on(phase, chunk, slot, values):
+    def scatter(chunk):
+        return [
+            pltpu.make_async_remote_copy(
+                src_ref=work[0].at[chunk, (chip + step) % chips],
+                dst_ref=landed.at[chunk - halved, step - 1],
+                send_sem=far_send.at[chunk - halved, step - 1],
+                recv_sem=far_recv.at[chunk - halved, step - 1],
+                device_id=far[step - 1],
+                device_id_type=MESH,
+            )
+            for step in range(1, chips)
+        ]
+
+    def join_scattered(chunk):
+        for copy in scatter(chunk):
+            copy.wait_recv()
+        for row in range(per_chunk):
+            running = [work[0][chunk, chip, rank, row] for rank in range(KEPT)]
+            for step in range(chips - 1):
+                running = merge_groups(running, [landed[chunk - halved, step, rank, row] for rank in range(KEPT)])
+            hand_on(bits, chunk, 0, running, row)
+
+    def hand_on(phase, chunk, slot, values, row):
         if phase < bits:
             for rank in range(KEPT):
-                work[phase][chunk, slot, rank] = values[rank]
+                work[phase][chunk, slot, rank, row] = values[rank]
             return
         values[TOP] = values[TOP] / math.sqrt(groups * local_tmpl)
         for rank in range(KEPT):
-            packed_ref[rank, pl.ds(chunk * per_chunk, per_chunk)] = values[rank]
-
-    def join_pair(chunk):
-        exchange(chunk).wait_recv()
-        for pair in range(chips):
-            former = [leaders[chunk, core, pair, rank] for rank in range(KEPT)]
-            latter = [sibling[chunk, pair, rank] for rank in range(KEPT)]
-            hand_on(0, chunk, shuffled(chips, chunk, pair), merge_groups(former, latter))
-        if bits:
-            halving(0, chunk).start()
+            packed_ref[rank, chunk * per_chunk + row] = values[rank]
 
     def join_far(phase, chunk):
         halving(phase, chunk).wait_recv()
         kept = chips >> (phase + 1)
         mine = own_bit(bit_order(chips, chunk)[phase]) * kept
         for slot in range(kept):
-            former = [work[phase][chunk, mine + slot, rank] for rank in range(KEPT)]
-            latter = [arrived[phase][chunk, slot, rank] for rank in range(KEPT)]
-            hand_on(phase + 1, chunk, slot, merge_groups(former, latter))
+            for row in range(per_chunk):
+                former = [work[phase][chunk, mine + slot, rank, row] for rank in range(KEPT)]
+                latter = [arrived[phase][chunk, slot, rank, row] for rank in range(KEPT)]
+                hand_on(phase + 1, chunk, slot, merge_groups(former, latter), row)
         if phase + 1 < bits:
             halving(phase + 1, chunk).start()
 
-    count = len(parts) - 1
-    for part in range(count):
+    late_numbers = range(late // STEP, local_tmpl // STEP)
+    for part in range(count - 1):
         lax.fori_loop(parts[part] // STEP, parts[part + 1] // STEP, transform, 0)
         if part == 0:
-            pl.semaphore_wait(barrier, 1 + len(across) + len(near))
+            pl.semaphore_wait(barrier, len(far) + len(near) + len(beside))
         publish(part)
+    for number in late_numbers:
+        transform(number, 0)
+        if number == late_numbers[-1]:
+            publish(count - 1)
+            for copy in tell_late():
+                copy.start()
+        for copy in raw(number, 1 - core):
+            copy.start()
     for part in range(count - 1):
         settle(part)
         for chunk in range(chunks):
             leading(part, chunk)
+            if part == count - 2:
+                exchange(chunk).start()
+    for number in late_numbers:
+        for copy in raw(number, core):
+            copy.wait_recv()
+    for chunk in range(chunks):
+        exchange(chunk).wait_recv()
     settle(count - 1)
     for chunk in range(chunks):
-        leading(count - 1, chunk)
-        exchange(chunk).start()
-        if chunk >= LAG:
-            join_pair(chunk - LAG)
-    for chunk in range(max(chunks - LAG, 0), chunks):
-        join_pair(chunk)
-    for phase in range(bits):
-        for chunk in range(chunks):
-            join_far(phase, chunk)
+        last_leading(chunk)
     for part in range(count):
         for copy in share_stats(part):
             copy.wait_send()
+    for copy in tell_late():
+        copy.wait_send()
+    for number in late_numbers:
+        for copy in raw(number, 1 - core):
+            copy.wait_send()
     for chunk in range(chunks):
         exchange(chunk).wait_send()
-        for phase in range(bits):
+    for chunk in range(halved):
+        join_far(0, chunk)
+    for chunk in range(halved):
+        halving(0, chunk).wait_send()
+    for chunk in range(halved, chunks):
+        join_scattered(chunk)
+    for phase in range(1, bits):
+        for chunk in range(halved):
+            join_far(phase, chunk)
+    for chunk in range(halved, chunks):
+        for copy in scatter(chunk):
+            copy.wait_send()
+    for phase in range(1, bits):
+        for chunk in range(halved):
             halving(phase, chunk).wait_send()
 
 
@@ -318,8 +433,11 @@
     bits = bits_of(chips)
     piece = beta_rows // groups
     chunks = min(CHUNKS, half)
+    halved = min(HALVED, chunks // 2)
     per_chunk = half // chunks
-    parts = (0, local_tmpl // 4 * 3, local_tmpl)
+    parts = (0, local_tmpl // 2, local_tmpl)
+    late_size = parts[-1] - parts[-2]
+    spans = chips if piece % TILE == 0 else 1
     count = len(parts) - 1
     block = (KEPT, per_chunk, piece, doubled)
     f32 = jnp.float32
@@ -336,21 +454,30 @@
             pltpu.VMEM((2, local_tmpl, doubled), f32),
             pltpu.VMEM((count, TILE, doubled), f32),
             pltpu.VMEM((count, slabs - 1, TILE, doubled), f32),
-            pltpu.VMEM((local_tmpl, doubled), f32),
-            pltpu.VMEM((local_tmpl, doubled), f32),
+            pltpu.VMEM((local_tmpl + late_size, doubled), f32),
+            pltpu.VMEM((local_tmpl + late_size, doubled), f32),
             pltpu.VMEM((chunks, 2, chips) + block, f32),
             pltpu.VMEM((chunks, chips) + block, f32),
+            pltpu.VMEM((late_size, half, beta_rows, doubled), f32),
+            pltpu.VMEM((slabs, TILE, doubled), f32),
         ]
         + [pltpu.VMEM((chunks, chips >> phase) + block, f32) for phase in range(max(bits, 1))]
         + [pltpu.VMEM((chunks, chips >> (phase + 1)) + block, f32) for phase in range(bits)]
+        + [pltpu.VMEM((chunks - halved, chips - 1) + block, f32)]
         + [
             dma((local_tmpl // STEP,)),
             dma((count, slabs - 1)),
             dma((count, slabs - 1)),
+            dma((slabs,)),
+            dma((slabs,)),
+            dma((late_size // STEP, spans)),
+            dma((late_size // STEP, spans)),
             dma((chunks,)),
             dma((chunks,)),
-            dma((max(bits, 1), chunks)),
-            dma((max(bits, 1), chunks)),
+            dma((bits, chunks)),
+            dma((bits, chunks)),
+            dma((chunks - halved, chips - 1)),
+            dma((chunks - halved, chips - 1)),
         ],
         compiler_params=pltpu.CompilerParams(
             collective_id=0, has_side_effects=True, vmem_limit_bytes=48 * 1024 * 1024

time: 27.1 us -> 26.2 us (0.967)
  Pallas kernels: 26.3 us -> 25.4 us
    pallas_call x1, Pallas kernels: 25.5 us -> 24.6 us  [body(): pl.pallas_call(functools.partial(kernel, groups, slabs, parts, chunks), o...]
where the time goes in v2:
time: 26.2 us; the launch traced here: 26 us
  Pallas kernels  25.4 us (97%)
  between operations  0.64 us (2%)
    pallas_call x1, Pallas kernels, body(): pl.pallas_call(functools.partial(kernel, groups, slabs, parts, chunks), o...  24.6 us
    pallas_call x1, Pallas kernels, body(): pl.pallas_call(unpack, out_shape=(jax.ShapeDtypeStruct((TOP, slab_rows, p...  0.82 us

profile of v2, /device:TPU:0, one launch (start us, length us, event | category | flops | bytes accessed | tf_op | source)
XLA Modules:
  0.0 26.0 jit_solution(2147449062903918581)
XLA Ops:
  0.6 24.6 %shard_map.30.packed_ref = f32[5,8,8,128]{3,2,1,0:T(8,128)S(1)} custom-call(f32[32,16,64,128]{3,2,1,0:T(8,128)} %spectrum_ref.1), custom_call_target="tpu_custom_call" | custom-call | tf_op jit(solution)/shard_map/pallas_call | solution.py:445
  25.2 0.8 %shard_map.31 = (f32[4,16,8,64]{3,2,1,0:T(8,128)}, f32[16,8,64]{2,1,0:T(8,128)}) custom-call(f32[5,8,8,128]{3,2,1,0:T(8,128)S(1)} %shard_map.30.packed_ref), custom_call_target="tpu_custom_call" | custom-call | tf_op jit(solution)/shard_map/pallas_call | solution.py:486

commit v3 on v2

--- a/solution.py
+++ b/solution.py
@@ -13,7 +13,7 @@
 SPREAD_FLOOR = 0.25
 CHUNKS = 8
 HALVED = 4
-STEP = 4
+STEP = 8
 TILE = 8
 MB = 256
 MESH = pl.DeviceIdType.MESH
@@ -369,10 +369,10 @@
         publish(part)
     for number in late_numbers:
         transform(number, 0)
-        if number == late_numbers[-1]:
-            publish(count - 1)
-            for copy in tell_late():
-                copy.start()
+    publish(count - 1)
+    for copy in tell_late():
+        copy.start()
+    for number in late_numbers:
         for copy in raw(number, 1 - core):
             copy.start()
     for part in range(count - 1):

time: 26.2 us -> 25.9 us (0.989)
  Pallas kernels: 25.4 us -> 25.1 us
    pallas_call x1, Pallas kernels: 24.6 us -> 24.3 us  [body(): pl.pallas_call(functools.partial(kernel, groups, slabs, parts, chunks), o...]
where the time goes in v3:
time: 25.9 us; the launch traced here: 25.7 us
  Pallas kernels  25.1 us (97%)
  between operations  0.64 us (2%)
    pallas_call x1, Pallas kernels, body(): pl.pallas_call(functools.partial(kernel, groups, slabs, parts, chunks), o...  24.3 us
    pallas_call x1, Pallas kernels, body(): pl.pallas_call(unpack, out_shape=(jax.ShapeDtypeStruct((TOP, slab_rows, p...  0.82 us

profile of v3, /device:TPU:0, one launch (start us, length us, event | category | flops | bytes accessed | tf_op | source)
XLA Modules:
  0.0 25.7 jit_solution(5276112487297079554)
XLA Ops:
  0.6 24.3 %shard_map.30.packed_ref = f32[5,8,8,128]{3,2,1,0:T(8,128)S(1)} custom-call(f32[32,16,64,128]{3,2,1,0:T(8,128)} %spectrum_ref.1), custom_call_target="tpu_custom_call" | custom-call | tf_op jit(solution)/shard_map/pallas_call | solution.py:445
  24.9 0.8 %shard_map.31 = (f32[4,16,8,64]{3,2,1,0:T(8,128)}, f32[16,8,64]{2,1,0:T(8,128)}) custom-call(f32[5,8,8,128]{3,2,1,0:T(8,128)S(1)} %shard_map.30.packed_ref), custom_call_target="tpu_custom_call" | custom-call | tf_op jit(solution)/shard_map/pallas_call | solution.py:486
